TPU v7x, 512 devices: a whole 4x4x16 slice. The times are simulated.
512 devices in a mesh: group: 8 (over x, y_hi), vocab: 64 (over z, y_lo, core).
Axes of the slice: x: 4, y: 4 (y_hi: 2, y_lo: 2; y = y_hi * 2 + y_lo), z: 16, core: 2. Of those that a mesh axis runs over, the one named last changes fastest.
Arguments:
- table: bfloat16 [4608, 196608], P('vocab', 'group')
- hidden: bfloat16 [448, 4608], P(None, 'vocab')
- gain: bfloat16 [4608], P('vocab'), may hold values from 0.099609375 to 1.8984375
- ids: int32 [448], replicated, may hold values from 0 to 196607
Outputs:
- next_embed: bfloat16 [448, 4608], P(None, 'vocab')
- logprobs: float32 [448, 196608], P(None, ('group', 'vocab'))
- chosen: float32 [448], replicated
All inputs are finite; a program needn't handle non-finite values.
Results may differ from a plain program's by a relative error of at most 0.001.
Values may be sent and summed in bfloat16 or wider, within the bound.
No kernel may reach another device: no remote copies, remote signals or barrier semaphores. Data moves between devices by JAX's collectives and lax.ppermute only.
A program may use at most 64 MiB of HBM per device.

v0:
```python
import math
import jax
import jax.numpy as jnp
from jax import lax
from jax.sharding import Mesh
from jax.sharding import PartitionSpec as P

VOCAB = ("vocab_0", "vocab_1", "vocab_2")
GROUP = ("group_0", "group_1")
GROUP_VOCAB = ("group_0", "group_1", "vocab_0", "vocab_1", "vocab_2")


def gather_turned(arrays, axis, dims):
    turned = [jnp.moveaxis(a, dim, 0) for a, dim in zip(arrays, dims)]
    both = jnp.concatenate([t.reshape(len(t), -1) for t in turned], axis=1)
    out, at, done = (lax.all_gather(both, axis, axis=0, tiled=True), 0, [])
    for t, dim in zip(turned, dims):
        slab = out[:, at : at + t[0].size].reshape(-1, *t.shape[1:])
        done.append(jnp.moveaxis(slab, 0, dim))
        at += t[0].size
    return tuple(done)


def in_blocks(array, dim, size):
    before, after = (array.shape[:dim], array.shape[dim + 1 :])
    return jnp.moveaxis(array.reshape(*before, size, -1, *after), dim, 0)


def cut_rows(length, count):
    lap = length // count
    if lap >= 8:
        lap -= lap % 8
    return [lap * k for k in range(1, count)]


def in_order(blocks, dim):
    lengths = list(blocks.shape[1:])
    lengths[dim] *= blocks.shape[0]
    return jnp.moveaxis(blocks, 0, dim).reshape(lengths)


def several_exchanges(array, axis, pieces, split_dim, concat_dim):
    blocks = in_blocks(array, split_dim, lax.axis_size(axis))
    widest = max(range(1, max(2, blocks.ndim - 1)), key=lambda d: blocks.shape[d])
    done = []
    for slab in jnp.split(blocks, cut_rows(blocks.shape[widest], pieces), axis=widest):
        if slab.size:
            done.append(lax.all_to_all(slab, axis, split_axis=0, concat_axis=0, tiled=True))
    return in_order(jnp.concatenate(done, axis=widest), concat_dim)


def over_axes(array, axes):
    for axis in axes:
        array = lax.psum(array, axis)
    return array


def body(table, hidden, gain, ids):
    share, span_cols = table.shape
    groups_n = lax.axis_size(VOCAB)
    voc_cols = span_cols // groups_n
    width = share * groups_n
    group_index = lax.axis_index(GROUP)
    vocab_index = lax.axis_index(VOCAB)
    local_ids = ids - group_index * span_cols
    inside = jnp.logical_and(local_ids >= 0, local_ids < span_cols)
    found = jnp.take(table, jnp.clip(local_ids, 0, span_cols - 1), axis=1).astype(jnp.float32).T
    found = found * inside[:, None].astype(jnp.float32)
    embed_cols = lax.psum(found.astype(jnp.bfloat16), GROUP).astype(jnp.float32)
    next_embed = (embed_cols * math.sqrt(width)).astype(jnp.bfloat16)
    whole, gain_all = gather_turned((hidden, gain), VOCAB, (1, 0))
    states = whole.astype(jnp.float32)
    mean_sq = jnp.sum(states * states, axis=1, keepdims=True) / width
    normed = (states * gain_all.astype(jnp.float32) * lax.rsqrt(mean_sq + 1e-06)).astype(
        jnp.bfloat16
    )
    full_cols = several_exchanges(table, VOCAB, 2, 1, 0)
    logits = jnp.dot(normed, full_cols, preferred_element_type=jnp.float32)
    capped = 30.0 * jnp.tanh(logits / 30.0)
    first_col = (group_index * groups_n + vocab_index) * voc_cols
    offsets = ids - first_col
    columns = lax.broadcasted_iota(jnp.int32, capped.shape, 1)
    pick = jnp.sum(jnp.where(columns == offsets[:, None], capped, 0.0), axis=1)
    sums, picks = (
        over_axes(jnp.sum(jnp.exp(capped), axis=1), GROUP_VOCAB),
        over_axes(pick, GROUP_VOCAB),
    )
    log_total = jnp.log(sums)
    logprobs = capped - log_total[:, None]
    chosen = picks - log_total
    return (next_embed, logprobs, chosen)


def solution(mesh):
    torus = Mesh(
        mesh.devices.reshape(4, 2, 16, 2, 2),
        ("group_0", "group_1", "vocab_0", "vocab_1", "vocab_2"),
    )
    return jax.shard_map(
        body,
        mesh=torus,
        in_specs=(P(VOCAB, GROUP), P(None, VOCAB), P(VOCAB), P()),
        out_specs=(P(None, VOCAB), P(None, GROUP_VOCAB), P()),
        check_vma=False,
    )
```

profile of v0, /device:TPU:1, one launch (start us, length us, event | category | flops | bytes accessed | tf_op | source)
XLA Modules:
  0.0 301.4 jit_solution(11320559064461386992)
XLA Ops:
  7.2 2.8 copy.22
  9.9 0.2 split.8
  10.1 2.1 copy.19
  12.2 18.3 %all-to-all-start = ((bf16[64,32,384]{2,1,0:T(8,128)(2,1)}), bf16[64,32,384]{2,1,0:T(8,128)(2,1)}, u32[]{:S(2)}, u32[]{:S(2)}) async-start(bf16[64,32,384]{2,1,0:T(8,128)(2,1)} %copy.19), calls=%async_computation | async-start | bytes 3145728 | tf_op jit(solution)/shard_map/all_to_all | solution.py:48
  30.5 0.0 all-gather.2.cloned.1.call-start
  30.6 0.7 copy.18
  31.3 1.6 pad_maximum_fusion.1
  32.9 0.0 all-gather.2.cloned.1.call-update
  32.9 0.2 split.9
  33.1 2.4 copy.20
  35.6 79.7 %all-to-all-done = bf16[64,32,384]{2,1,0:T(8,128)(2,1)} async-done(((bf16[64,32,384]{2,1,0:T(8,128)(2,1)}), bf16[64,32,384]{2,1,0:T(8,128)(2,1)}, u32[]{:S(2)}, u32[]{:S(2)}) %all-to-all-start) | async-done | bytes 1572896 | tf_op jit(solution)/shard_map/all_to_all | solution.py:48
  115.3 6.8 %all-to-all-start.1 = ((bf16[64,40,384]{2,1,0:T(8,128)(2,1)}), bf16[64,40,384]{2,1,0:T(8,128)(2,1)}, u32[]{:S(2)}, u32[]{:S(2)}) async-start(bf16[64,40,384]{2,1,0:T(8,128)(2,1)} %copy.20), calls=%async_computation.1 | async-start | bytes 3932160 | tf_op jit(solution)/shard_map/all_to_all | solution.py:48
  122.1 0.0 copy-start.2
  122.1 5.3 %copy.17 = bf16[72,24576]{0,1:T(8,128)(2,1)} copy(bf16[72,24576]{1,0:T(8,128)(2,1)S(1)} %copy-done) | data formatting | bytes 7077888 | tf_op args[0]
  127.4 4.8 %gather_fusion = bf16[448,72]{1,0:T(8,128)(2,1)S(1)} fusion(bf16[72,24576]{0,1:T(8,128)(2,1)} %copy.17, s32[1024]{0:T(1024)S(1)} %pad_clamp_fusion), kind=kCustom, calls=%fused_computation | custom fusion | bytes 130816 | tf_op jit(solution)/shard_map/jit(_take)/gather | solution.py:67
  132.2 0.2 multiply_convert_fusion
  132.4 38.7 %psum.77 = bf16[448,72]{1,0:T(8,128)(2,1)S(1)} all-reduce(bf16[448,72]{1,0:T(8,128)(2,1)S(1)} %multiply_convert_fusion), channel_id=1, replica_groups=mesh['group_0'=4,'group_1'=2,'vocab_0'=16,'vocab_1'=2,'vocab_2'=2] {'gro..., use_global_device_ids=true, to_apply=%region_0.1 | all-reduce | flops 32256 | bytes 129024 | tf_op jit(solution)/shard_map/psum | solution.py:69
  171.1 0.7 copy.21
  171.9 55.3 %all-to-all-done.1 = bf16[64,40,384]{2,1,0:T(8,128)(2,1)} async-done(((bf16[64,40,384]{2,1,0:T(8,128)(2,1)}), bf16[64,40,384]{2,1,0:T(8,128)(2,1)}, u32[]{:S(2)}, u32[]{:S(2)}) %all-to-all-start.1) | async-done | bytes 1966112 | tf_op jit(solution)/shard_map/all_to_all | solution.py:48
  227.1 2.4 pad_maximum_fusion
  229.5 0.0 all-gather.2.cloned.1.call-done
  229.5 3.6 %fusion.2 = f32[448]{0:T(512)S(1)} fusion(bf16[4608,449]{1,0:T(8,128)(2,1)} %all-gather.2.cloned.1.call-done), kind=kLoop, calls=%fused_computation.5 | loop fusion | flops 6192704 | bytes 4130560 | tf_op jit(solution)/shard_map/reduce_sum | solution.py:73
  233.1 0.2 copy-done.1
  233.3 0.8 convert_reduce_fusion
  234.1 4.3 %select_reduce_fusion = (f32[448]{0:T(512)S(1)}, f32[448]{0:T(512)S(1)}, f32[448,384]{1,0:T(8,128)}) fusion(s32[448]{0:T(512)S(1)} %broadcast_subtract_fusion.1, bf16[4608,384]{1,0:T(8,128)(2,1)S(1)} %bitcast.11, f32[448]{0:T(512)S(1)} %add_rsqrt_fusion, f32[4608]{0:T(1024)S(1)} %convert_reduce_fusion, bf16[4608,449]{1,0:T(8,128)(2,1)S(1)} %copy-done.1), kind=kOutput, calls=%fused_computation.15 | convolution fusion | flops 1594735616 | bytes 8390656 | tf_op jit(solution)/shard_map/dot_general | solution.py:78
  238.4 8.3 %all-reduce.1 = (f32[448]{0:T(512)S(1)}, f32[448]{0:T(512)S(1)}) all-reduce(f32[448]{0:T(512)S(1)} %get-tuple-element.16, f32[448]{0:T(512)S(1)} %get-tuple-element.15), channel_id=1, replica_groups=mesh['group_0'=4,'group_1'=2,'vocab_0'=16,'vocab_1'=2,'vocab_2'=2] {'gro..., use_global_device_ids=true, to_apply=%region_3.4 | all-reduce | flops 896 | bytes 7168 | tf_op jit(solution)/shard_map/psum | solution.py:54
  246.8 5.5 %all-reduce.4 = (f32[448]{0:T(512)S(1)}, f32[448]{0:T(512)S(1)}) all-reduce(f32[448]{0:T(512)S(1)} %get-tuple-element.19, f32[448]{0:T(512)S(1)} %get-tuple-element.20), channel_id=1, replica_groups=mesh['group_0'=4,'group_1'=2,'vocab_0'=16,'vocab_1'=2,'vocab_2'=2] {'gro..., use_global_device_ids=true, to_apply=%region_4.5 | all-reduce | flops 896 | bytes 7168 | tf_op jit(solution)/shard_map/psum | solution.py:54
  252.3 22.0 %all-reduce = (f32[448]{0:T(512)S(1)}, f32[448]{0:T(512)S(1)}) all-reduce(f32[448]{0:T(512)S(1)} %get-tuple-element.25, f32[448]{0:T(512)S(1)} %get-tuple-element.26), channel_id=1, replica_groups=mesh['group_0'=4,'group_1'=2,'vocab_0'=16,'vocab_1'=2,'vocab_2'=2] {'voc..., use_global_device_ids=true, to_apply=%region_5.6 | all-reduce | flops 896 | bytes 7168 | tf_op jit(solution)/shard_map/psum | solution.py:54
  274.3 3.8 %all-reduce.3 = (f32[448]{0:T(512)S(1)}, f32[448]{0:T(512)S(1)}) all-reduce(f32[448]{0:T(512)S(1)} %get-tuple-element.17, f32[448]{0:T(512)S(1)} %get-tuple-element.18), channel_id=1, replica_groups=mesh['group_0'=4,'group_1'=2,'vocab_0'=16,'vocab_1'=2,'vocab_2'=2] {'voc..., use_global_device_ids=true, to_apply=%region_6.7 | all-reduce | flops 896 | bytes 7168 | tf_op jit(solution)/shard_map/psum | solution.py:54
  278.1 13.8 %all-reduce.2 = (f32[448]{0:T(512)S(1)}, f32[448]{0:T(512)S(1)}) all-reduce(f32[448]{0:T(512)S(1)} %get-tuple-element.23, f32[448]{0:T(512)S(1)} %get-tuple-element.24), channel_id=1, replica_groups=mesh['group_0'=4,'group_1'=2,'vocab_0'=16,'vocab_1'=2,'vocab_2'=2] {'voc..., use_global_device_ids=true, to_apply=%region_7.8 | all-reduce | flops 896 | bytes 7168 | tf_op jit(solution)/shard_map/psum | solution.py:54
  291.9 0.6 log_subtract_fusion
  292.5 2.1 broadcast_subtract_fusion
  (11 shorter events, 0.1 us)
Async XLA Ops:
  9.9 20.6 %copy-start.3 = (bf16[72]{0:T(256)(128)(2,1)S(1)}, bf16[72]{0:T(256)(128)(2,1)}, u32[]{:S(2)}) copy-start(bf16[72]{0:T(256)(128)(2,1)} %param.6) | copy-start | bytes 436
  12.2 103.1 %all-to-all-start = ((bf16[64,32,384]{2,1,0:T(8,128)(2,1)}), bf16[64,32,384]{2,1,0:T(8,128)(2,1)}, u32[]{:S(2)}, u32[]{:S(2)}) async-start(bf16[64,32,384]{2,1,0:T(8,128)(2,1)} %copy.19), calls=%async_computation | async-start | bytes 3145728 | tf_op jit(solution)/shard_map/all_to_all | solution.py:48
  30.5 199.0 %all-gather.2.cloned.1.call-start = ((), (), s32[]{:S(2)}) async-start(), calls=%async_computation.2 | async-start | bytes 4792320 | tf_op jit(solution)/shard_map/all_gather | solution.py:16
  33.1 89.0 %copy-start = (bf16[72,24576]{1,0:T(8,128)(2,1)S(1)}, bf16[72,24576]{1,0:T(8,128)(2,1)}, u32[]{:S(2)}) copy-start(bf16[72,24576]{1,0:T(8,128)(2,1)} %param.4) | copy-start | bytes 10616836
  115.3 111.9 %all-to-all-start.1 = ((bf16[64,40,384]{2,1,0:T(8,128)(2,1)}), bf16[64,40,384]{2,1,0:T(8,128)(2,1)}, u32[]{:S(2)}, u32[]{:S(2)}) async-start(bf16[64,40,384]{2,1,0:T(8,128)(2,1)} %copy.20), calls=%async_computation.1 | async-start | bytes 3932160 | tf_op jit(solution)/shard_map/all_to_all | solution.py:48
  122.1 5.3 %copy-start.2 = (s32[448]{0:T(512)S(1)}, s32[448]{0:T(512)}, u32[]{:S(2)}) copy-start(s32[448]{0:T(512)} %param.7) | copy-start | bytes 5380
  229.5 3.8 %copy-start.1 = (bf16[4608,449]{1,0:T(8,128)(2,1)S(1)}, bf16[4608,449]{1,0:T(8,128)(2,1)}, u32[]{:S(2)}) copy-start(bf16[4608,449]{1,0:T(8,128)(2,1)} %all-gather.2.cloned.1.call-done) | copy-start | bytes 12413956
Sparse Core Ops, SparseCore 0:
  34.0 191.4 all-gather.1
where the time goes:
time: 302 us; the launch traced here: 301 us
  waiting for transfers between devices  135 us (45%)
  blocking collectives  92.1 us (30%)
  starting transfers between devices  25.2 us (8%)
  local copies, waits for them, and re-layouts  19.4 us (6%)
  between operations  14.2 us (5%)
  other arithmetic  11.3 us (4%)
  matrix products  4.32 us (1%)
    all_to_all x2, waiting for transfers between devices, several_exchanges(): lax.all_to_all(slab, axis, split_axis=0, concat_axis=0, tiled=True)  135 us
    psum x5, blocking collectives, over_axes(): array = lax.psum(array, axis)  53.4 us
    psum x1, blocking collectives, body(): embed_cols = lax.psum(found.astype(jnp.bfloat16), GROUP).astype(jnp.float32)  38.7 us
    all_to_all x2, starting transfers between devices, several_exchanges(): lax.all_to_all(slab, axis, split_axis=0, concat_axis=0, tiled=True)  25.1 us
    unnamed x11, local copies, waits for them, and re-layouts  8.96 us
  transfers between devices with their start and end apart: 3, of which 2 were waited for; matrix products, arithmetic and copies ran while one was open for 6% of the time, Pallas kernels for 0%

commit v1 on v0

--- a/solution.py
+++ b/solution.py
@@ -51,7 +51,7 @@
 
 def over_axes(array, axes):
     for axis in axes:
-        array = lax.psum(array, axis)
+        array = jnp.sum(lax.all_gather(array, axis), axis=0)
     return array
 
 

time: 302 us -> 337 us (1.12)
  blocking collectives: 92.1 us -> 124 us
  local copies, waits for them, and re-layouts: 19.4 us -> 28.9 us
  waiting for transfers between devices: 135 us -> 126 us
    unnamed x0 -> x5, blocking collectives: none -> 85.3 us
    psum x5 -> x0, blocking collectives: 53.4 us -> none  [over_axes(): array = lax.psum(array, axis)]
    all_to_all x2, waiting for transfers between devices: 135 us -> 126 us  [several_exchanges(): lax.all_to_all(slab, axis, split_axis=0, concat_axis=0, tiled=True)]
    unnamed x11 -> x36, local copies, waits for them, and re-layouts: 8.96 us -> 17.7 us
  transfers between devices with their start and end apart: 3 -> 3, of which waited for: 2 -> 2; matrix products, arithmetic and copies ran while one was open for 6% -> 7% of each run, Pallas kernels for 0% -> 0%
where the time goes in v1:
time: 337 us
  waiting for transfers between devices  126 us (37%)
  blocking collectives  124 us (37%)
  local copies, waits for them, and re-layouts  28.9 us (9%)
  starting transfers between devices  25.2 us (7%)
  between operations  17.5 us (5%)
  other arithmetic  11.5 us (3%)
  matrix products  4.32 us (1%)
    all_to_all x2, waiting for transfers between devices, several_exchanges(): lax.all_to_all(slab, axis, split_axis=0, concat_axis=0, tiled=True)  126 us
    unnamed x5, blocking collectives  85.3 us
    psum x1, blocking collectives, body(): embed_cols = lax.psum(found.astype(jnp.bfloat16), GROUP).astype(jnp.float32)  38.6 us
    all_to_all x2, starting transfers between devices, several_exchanges(): lax.all_to_all(slab, axis, split_axis=0, concat_axis=0, tiled=True)  25.1 us
    unnamed x36, local copies, waits for them, and re-layouts  17.7 us
  transfers between devices with their start and end apart: 3, of which 2 were waited for; matrix products, arithmetic and copies ran while one was open for 7% of the time, Pallas kernels for 0%

profile of v1, /device:TPU:1, one launch (start us, length us, event | category | flops | bytes accessed | tf_op | source)
XLA Modules:
  0.0 336.7 jit_solution(7143466322642679538)
XLA Ops:
  7.2 2.8 copy.27
  10.1 2.1 copy.24
  12.2 18.3 %all-to-all-start = ((bf16[64,32,384]{2,1,0:T(8,128)(2,1)}), bf16[64,32,384]{2,1,0:T(8,128)(2,1)}, u32[]{:S(2)}, u32[]{:S(2)}) async-start(bf16[64,32,384]{2,1,0:T(8,128)(2,1)} %copy.24), calls=%async_computation | async-start | bytes 3145728 | tf_op jit(solution)/shard_map/all_to_all | solution.py:48
  30.6 0.7 copy.23
  31.3 1.6 pad_maximum_fusion.1
  33.1 2.4 copy.25
  35.6 79.7 %all-to-all-done = bf16[64,32,384]{2,1,0:T(8,128)(2,1)} async-done(((bf16[64,32,384]{2,1,0:T(8,128)(2,1)}), bf16[64,32,384]{2,1,0:T(8,128)(2,1)}, u32[]{:S(2)}, u32[]{:S(2)}) %all-to-all-start) | async-done | bytes 1572896 | tf_op jit(solution)/shard_map/all_to_all | solution.py:48
  115.3 6.8 %all-to-all-start.1 = ((bf16[64,40,384]{2,1,0:T(8,128)(2,1)}), bf16[64,40,384]{2,1,0:T(8,128)(2,1)}, u32[]{:S(2)}, u32[]{:S(2)}) async-start(bf16[64,40,384]{2,1,0:T(8,128)(2,1)} %copy.25), calls=%async_computation.1 | async-start | bytes 3932160 | tf_op jit(solution)/shard_map/all_to_all | solution.py:48
  122.1 5.3 %copy.22 = bf16[72,24576]{0,1:T(8,128)(2,1)} copy(bf16[72,24576]{1,0:T(8,128)(2,1)S(1)} %copy-done) | data formatting | bytes 7077888 | tf_op args[0]
  127.4 1.3 dynamic-slice
  128.6 1.3 dynamic-slice.1
  131.2 1.3 dynamic-slice.2
  133.1 1.3 dynamic-slice.3
  135.1 1.3 dynamic-slice.4
  137.0 4.8 %gather_fusion = bf16[448,72]{1,0:T(8,128)(2,1)S(1)} fusion(bf16[72,24576]{0,1:T(8,128)(2,1)} %copy.22, s32[1024]{0:T(1024)S(1)} %pad_clamp_fusion), kind=kCustom, calls=%fused_computation | custom fusion | bytes 130816 | tf_op jit(solution)/shard_map/jit(_take)/gather | solution.py:67
  142.0 38.6 %psum.7 = bf16[448,72]{1,0:T(8,128)(2,1)S(1)} all-reduce(bf16[448,72]{1,0:T(8,128)(2,1)S(1)} %multiply_convert_fusion), channel_id=1, replica_groups=mesh['group_0'=4,'group_1'=2,'vocab_0'=16,'vocab_1'=2,'vocab_2'=2] {'gro..., use_global_device_ids=true, to_apply=%region_0.1 | all-reduce | flops 32256 | bytes 129024 | tf_op jit(solution)/shard_map/psum | solution.py:69
  180.7 0.7 copy.26
  181.4 45.9 %all-to-all-done.1 = bf16[64,40,384]{2,1,0:T(8,128)(2,1)} async-done(((bf16[64,40,384]{2,1,0:T(8,128)(2,1)}), bf16[64,40,384]{2,1,0:T(8,128)(2,1)}, u32[]{:S(2)}, u32[]{:S(2)}) %all-to-all-start.1) | async-done | bytes 1966112 | tf_op jit(solution)/shard_map/all_to_all | solution.py:48
  227.3 2.4 pad_maximum_fusion
  229.7 3.6 %fusion.2 = f32[448]{0:T(512)S(1)} fusion(bf16[4608,449]{1,0:T(8,128)(2,1)} %all-gather.12.cloned.1.call-done), kind=kLoop, calls=%fused_computation.5 | loop fusion | flops 6192704 | bytes 4130560 | tf_op jit(solution)/shard_map/reduce_sum | solution.py:73
  233.4 0.8 convert_reduce_fusion
  234.2 4.3 %select_reduce_fusion = (f32[448]{0:T(512)S(1)}, f32[448]{0:T(512)S(1)}, f32[448,384]{1,0:T(8,128)}) fusion(s32[448]{0:T(512)S(1)} %broadcast_subtract_fusion.1, bf16[4608,384]{1,0:T(8,128)(2,1)S(1)} %bitcast.16, f32[448]{0:T(512)S(1)} %add_rsqrt_fusion, f32[4608]{0:T(1024)S(1)} %convert_reduce_fusion, bf16[4608,449]{1,0:T(8,128)(2,1)S(1)} %copy-done.1), kind=kOutput, calls=%fused_computation.15 | convolution fusion | flops 1594735616 | bytes 8390656 | tf_op jit(solution)/shard_map/dot_general | solution.py:78
  238.8 0.3 dynamic-update-slice.5
  239.0 12.9 %all-reduce.11 = (f32[1792]{0:T(1024)S(1)}, f32[1792]{0:T(1024)S(1)}) all-reduce(f32[1792]{0:T(1024)S(1)} %dynamic-update-slice, f32[1792]{0:T(1024)S(1)} %dynamic-update-slice.5), channel_id=2, replica_groups=mesh['group_0'=4,'group_1'=2,'vocab_0'=16,'vocab_1'=2,'vocab_2'=2] {'gro..., use_global_device_ids=true, to_apply=%add | all-reduce | flops 3584 | bytes 28672
  252.5 5.3 %all-reduce.14 = (f32[896]{0:T(1024)S(1)}, f32[896]{0:T(1024)S(1)}) all-reduce(f32[896]{0:T(1024)S(1)} %dynamic-update-slice.1, f32[896]{0:T(1024)S(1)} %dynamic-update-slice.6), channel_id=3, replica_groups=mesh['group_0'=4,'group_1'=2,'vocab_0'=16,'vocab_1'=2,'vocab_2'=2] {'gro..., use_global_device_ids=true, to_apply=%add.1 | all-reduce | flops 1792 | bytes 14336
  258.1 0.3 dynamic-update-slice.7
  258.3 0.3 dynamic-update-slice.2
  258.6 41.0 %all-reduce.10 = (f32[7168]{0:T(1024)S(1)}, f32[7168]{0:T(1024)S(1)}) all-reduce(f32[7168]{0:T(1024)S(1)} %dynamic-update-slice.2, f32[7168]{0:T(1024)S(1)} %dynamic-update-slice.7), channel_id=4, replica_groups=mesh['group_0'=4,'group_1'=2,'vocab_0'=16,'vocab_1'=2,'vocab_2'=2] {'voc..., use_global_device_ids=true, to_apply=%add.2 | all-reduce | flops 14336 | bytes 114688
  300.3 3.8 %all-reduce.13 = (f32[896]{0:T(1024)S(1)}, f32[896]{0:T(1024)S(1)}) all-reduce(f32[896]{0:T(1024)S(1)} %dynamic-update-slice.3, f32[896]{0:T(1024)S(1)} %dynamic-update-slice.8), channel_id=5, replica_groups=mesh['group_0'=4,'group_1'=2,'vocab_0'=16,'vocab_1'=2,'vocab_2'=2] {'voc..., use_global_device_ids=true, to_apply=%add.3 | all-reduce | flops 1792 | bytes 14336
  304.7 22.3 %all-reduce.12 = (f32[896]{0:T(1024)S(1)}, f32[896]{0:T(1024)S(1)}) all-reduce(f32[896]{0:T(1024)S(1)} %dynamic-update-slice.4, f32[896]{0:T(1024)S(1)} %dynamic-update-slice.9), channel_id=6, replica_groups=mesh['group_0'=4,'group_1'=2,'vocab_0'=16,'vocab_1'=2,'vocab_2'=2] {'voc..., use_global_device_ids=true, to_apply=%add.4 | all-reduce | flops 1792 | bytes 14336
  327.2 0.6 log_subtract_fusion
  327.8 2.1 broadcast_subtract_fusion
  (56 shorter events, 3.4 us)
Async XLA Ops:
  9.9 20.6 %copy-start.3 = (bf16[72]{0:T(256)(128)(2,1)S(1)}, bf16[72]{0:T(256)(128)(2,1)}, u32[]{:S(2)}) copy-start(bf16[72]{0:T(256)(128)(2,1)} %param.6) | copy-start | bytes 436
  12.2 103.1 %all-to-all-start = ((bf16[64,32,384]{2,1,0:T(8,128)(2,1)}), bf16[64,32,384]{2,1,0:T(8,128)(2,1)}, u32[]{:S(2)}, u32[]{:S(2)}) async-start(bf16[64,32,384]{2,1,0:T(8,128)(2,1)} %copy.24), calls=%async_computation | async-start | bytes 3145728 | tf_op jit(solution)/shard_map/all_to_all | solution.py:48
  30.5 199.1 %all-gather.12.cloned.1.call-start = ((), (), s32[]{:S(2)}) async-start(), calls=%async_computation.2 | async-start | bytes 4792320 | tf_op jit(solution)/shard_map/all_gather | solution.py:16
  33.1 89.0 %copy-start = (bf16[72,24576]{1,0:T(8,128)(2,1)S(1)}, bf16[72,24576]{1,0:T(8,128)(2,1)}, u32[]{:S(2)}) copy-start(bf16[72,24576]{1,0:T(8,128)(2,1)} %param.4) | copy-start | bytes 10616836
  115.3 112.0 %all-to-all-start.1 = ((bf16[64,40,384]{2,1,0:T(8,128)(2,1)}), bf16[64,40,384]{2,1,0:T(8,128)(2,1)}, u32[]{:S(2)}, u32[]{:S(2)}) async-start(bf16[64,40,384]{2,1,0:T(8,128)(2,1)} %copy.25), calls=%async_computation.1 | async-start | bytes 3932160 | tf_op jit(solution)/shard_map/all_to_all | solution.py:48
  122.1 14.9 %copy-start.2 = (s32[448]{0:T(512)S(1)}, s32[448]{0:T(512)}, u32[]{:S(2)}) copy-start(s32[448]{0:T(512)} %param.7) | copy-start | bytes 5380
  229.7 3.8 %copy-start.1 = (bf16[4608,449]{1,0:T(8,128)(2,1)S(1)}, bf16[4608,449]{1,0:T(8,128)(2,1)}, u32[]{:S(2)}) copy-start(bf16[4608,449]{1,0:T(8,128)(2,1)} %all-gather.12.cloned.1.call-done) | copy-start | bytes 12413956
Sparse Core Ops, SparseCore 0:
  34.0 191.6 all-gather.11
